TPU v7x, 512 devices: a whole 4x8x8 slice. The times are simulated.
512 devices in a mesh: tm: 16 (over y, core), rows: 32 (over z, x).
Axes of the slice: x: 4, y: 8, z: 8, core: 2. Of those that a mesh axis runs over, the one named last changes fastest.
Arguments:
- features: bfloat16 [16, 96, 64, 512], P('tm', 'rows'), may hold values from -64 to 64, as said below
- gamma: float32 [512], replicated, may hold values from 0.1 to 1.9
- beta: float32 [512], replicated, may hold values from -3 to 3
- kernel: bfloat16 [3, 512, 3, 3, 512], P(None, 'tm'), may hold values from -0.0546875 to 0.0546875
- bias: float32 [512], replicated, may hold values from -3 to 3
Outputs:
- decoded: bfloat16 [16, 96, 64, 512], P('tm', 'rows')
Inputs may be any that keep to these rules, and one draw needn't show every extreme that they name: features are finite.
All inputs are finite; a program needn't handle non-finite values.
Results may differ from a plain program's by a relative error of at most 0.004.
Values may be sent and summed in bfloat16 or wider, within the bound.
A program may use at most 128 MiB of HBM per device.

v0:
```python
import functools

import jax
import jax.numpy as jnp
from jax import lax
from jax.sharding import Mesh
from jax.sharding import PartitionSpec as P

GROUPS = 32
TM = ("tm_0", "tm_1")
ROWS = ("rows_0", "rows_1")
TM_ROWS = ("tm_0", "tm_1", "rows_0", "rows_1")


EPSILON = 1e-06


def shifted(x, axis, by):
    length = lax.axis_size(axis)
    pairs = [(i, i + by) for i in range(length) if 0 <= i + by < length]
    return lax.ppermute(x, axis, pairs)


def one_axis_at_a_time(x, axes):
    return functools.reduce(lax.psum, axes, x)


def extended_2(x, sides, width):
    for axis, dim in sides:
        size, length = (lax.axis_size(axis), x.shape[dim])
        up = [(i, (i + 1) % size) for i in range(size - 1)]
        down = [(j, i) for i, j in up]
        last = lax.slice_in_dim(x, length - width, length, axis=dim)
        first = lax.slice_in_dim(x, 0, width, axis=dim)
        before = lax.ppermute(last, axis, up)
        after = lax.ppermute(first, axis, down)
        x = jnp.concatenate([before, x, after], axis=dim)
    return x


def unfold(block, height, across):
    pieces = []
    for tap_row in range(3):
        for tap_col in range(3):
            pieces.append(block[:, tap_row : tap_row + height, tap_col : tap_col + across, :])
    return jnp.concatenate(pieces, axis=-1)


def flatten_taps(taps):
    return taps.reshape(3, taps.shape[1], -1)


def apply_taps(columns, taps, frames):
    flat = flatten_taps(taps)
    total = jnp.einsum(
        "fhwc,kc->fhwk", columns[0:frames], flat[0], preferred_element_type=jnp.float32
    )
    for tap_time in (1, 2):
        total = total + jnp.einsum(
            "fhwc,kc->fhwk",
            columns[tap_time : tap_time + frames],
            flat[tap_time],
            preferred_element_type=jnp.float32,
        )
    return total


def widen(block):
    return jnp.pad(block, ((0, 0), (0, 0), (1, 1), (0, 0)))


def previous_span(block):
    return shifted(block, TM, 1)


def local(features, gamma, beta, kernel, bias):
    frames, height, across, channels = features.shape
    values = features.astype(jnp.float32)
    grouped = values.reshape(frames, height, across, GROUPS, channels // GROUPS)
    count = float(
        frames * height * across * (channels // GROUPS) * lax.axis_size(TM) * lax.axis_size(ROWS)
    )
    totals, squares = (
        one_axis_at_a_time(jnp.sum(grouped, axis=(0, 1, 2, 4)), TM_ROWS),
        one_axis_at_a_time(jnp.sum(grouped * grouped, axis=(0, 1, 2, 4)), TM_ROWS),
    )
    center = totals / count
    spread = squares / count - center * center
    centered = grouped - center[:, None]
    normed = (centered * lax.rsqrt(spread + EPSILON)[:, None]).reshape(
        frames, height, across, channels
    )
    active = jax.nn.silu(normed * gamma + beta).astype(jnp.bfloat16)
    rimmed = extended_2(active, ((ROWS, 1),), 1)
    first_span = lax.axis_index(TM) == 0
    minus_one = jnp.where(first_span, rimmed, previous_span(rimmed))
    minus_two = jnp.where(first_span, rimmed, previous_span(minus_one))
    cache = jnp.concatenate([minus_two, minus_one], axis=0)
    extended = widen(jnp.concatenate([cache, rimmed], axis=0))
    columns = unfold(extended, height, across)
    conv = apply_taps(columns, lax.all_gather(kernel, TM, axis=1, tiled=True), frames)
    return (values + conv + bias).astype(jnp.bfloat16)


def solution(mesh):
    split = Mesh(mesh.devices.reshape(8, 2, 8, 4), ("tm_0", "tm_1", "rows_0", "rows_1"))
    in_specs = (P(TM, ROWS, None, None), P(), P(), P(None, TM, None, None, None), P())
    out_specs = P(TM, ROWS, None, None)
    return jax.shard_map(local, mesh=split, in_specs=in_specs, out_specs=out_specs, check_vma=False)
```

profile of v0, /device:TPU:1, one launch (start us, length us, event | category | flops | bytes accessed | tf_op | source)
XLA Modules:
  0.0 159.1 jit_solution(3659426236268656554)
XLA Ops:
  6.5 0.0 all-gather.2.cloned.1.call-start
  6.5 0.7 all-gather.2.cloned.1.call-update
  7.3 1.0 convert_reduce_fusion
  8.3 0.1 reduce_sum.36
  8.3 0.1 reduce_sum.24
  8.4 0.1 reduce_sum.37
  8.5 0.1 reduce_sum.25
  8.7 14.7 %all-reduce.2 = (f32[32]{0:T(128)S(1)}, f32[32]{0:T(128)S(1)}) all-reduce(f32[32]{0:T(128)S(1)} %reduce_sum.37, f32[32]{0:T(128)S(1)} %reduce_sum.25), channel_id=1, replica_groups=mesh['tm_0'=8,'tm_1'=2,'rows_0'=8,'rows_1'=4] {'tm_0'}, use_global_device_ids=true, to_apply=%region_8.0 | all-reduce | flops 64 | bytes 512 | tf_op jit(solution)/shard_map/psum | solution.py:25
  23.3 8.4 %all-reduce.4 = (f32[32]{0:T(128)S(1)}, f32[32]{0:T(128)S(1)}) all-reduce(f32[32]{0:T(128)S(1)} %get-tuple-element.9, f32[32]{0:T(128)S(1)} %get-tuple-element.10), channel_id=1, replica_groups=mesh['tm_0'=8,'tm_1'=2,'rows_0'=8,'rows_1'=4] {'tm_1'}, use_global_device_ids=true, to_apply=%region_9.0 | all-reduce | flops 64 | bytes 512 | tf_op jit(solution)/shard_map/psum | solution.py:25
  31.8 19.1 %all-reduce.1 = (f32[32]{0:T(128)S(1)}, f32[32]{0:T(128)S(1)}) all-reduce(f32[32]{0:T(128)S(1)} %get-tuple-element.13, f32[32]{0:T(128)S(1)} %get-tuple-element.14), channel_id=1, replica_groups=mesh['tm_0'=8,'tm_1'=2,'rows_0'=8,'rows_1'=4] {'rows_0'}, use_global_device_ids=true, to_apply=%region_10.11 | all-reduce | flops 64 | bytes 512 | tf_op jit(solution)/shard_map/psum | solution.py:25
  50.9 9.3 %all-reduce.3 = (f32[32]{0:T(128)S(1)}, f32[32]{0:T(128)S(1)}) all-reduce(f32[32]{0:T(128)S(1)} %get-tuple-element.7, f32[32]{0:T(128)S(1)} %get-tuple-element.8), channel_id=1, replica_groups=mesh['tm_0'=8,'tm_1'=2,'rows_0'=8,'rows_1'=4] {'rows_1'}, use_global_device_ids=true, to_apply=%region_11.12 | all-reduce | flops 64 | bytes 512 | tf_op jit(solution)/shard_map/psum | solution.py:25
  60.2 0.1 mul.47
  60.3 0.1 mul.48
  60.3 0.1 sub.19
  60.4 0.1 sub.20
  60.5 1.1 fusion.23
  61.6 1.3 collective-permute-start.1
  62.9 4.0 %collective-permute-start = (bf16[1,1,64,512]{3,2,1,0:T(8,128)(2,1)S(1)}, bf16[1,1,64,512]{3,2,1,0:T(8,128)(2,1)S(1)}, u32[]{:S(2)}, u32[]{:S(2)}) collective-permute-start(bf16[1,1,64,512]{3,2,1,0:T(8,128)(2,1)S(1)} %get-tuple-element.18), channel_id=1, source_target_pairs={{0,1},{1,2},{2,3},{3,4},{4,5},{5,6},{6,7},{7,8},{8,9},{9,10},{10,1... | collective-permute-start | bytes 196616 | tf_op jit(solution)/shard_map/ppermute | solution.py:35
  66.9 0.1 collective-permute-done.1
  67.0 1.2 collective-permute-done
  68.3 6.5 %collective-permute-start.2 = (bf16[1,5,64,512]{3,2,1,0:T(8,128)(2,1)S(1)}, bf16[1,5,64,512]{3,2,1,0:T(8,128)(2,1)S(1)}, u32[]{:S(2)}, u32[]{:S(2)}) collective-permute-start(bf16[1,5,64,512]{3,2,1,0:T(8,128)(2,1)S(1)} %pad_maximum_fusion), channel_id=1, source_target_pairs={{0,32},{32,64},{64,96},{96,128},{128,160},{160,192},{192,224},{224... | collective-permute-start | bytes 983048 | tf_op jit(solution)/shard_map/ppermute | solution.py:21
  74.8 11.1 %collective-permute-done.2 = bf16[1,5,64,512]{3,2,1,0:T(8,128)(2,1)S(1)} collective-permute-done((bf16[1,5,64,512]{3,2,1,0:T(8,128)(2,1)S(1)}, bf16[1,5,64,512]{3,2,1,0:T(8,128)(2,1)S(1)}, u32[]{:S(2)}, u32[]{:S(2)}) %collective-permute-start.2) | collective-permute-done | bytes 327712 | tf_op jit(solution)/shard_map/ppermute | solution.py:21
  86.0 4.4 %collective-permute-start.3 = (bf16[1,5,64,512]{3,2,1,0:T(8,128)(2,1)S(1)}, bf16[1,5,64,512]{3,2,1,0:T(8,128)(2,1)S(1)}, u32[]{:S(2)}, u32[]{:S(2)}) collective-permute-start(bf16[1,5,64,512]{3,2,1,0:T(8,128)(2,1)S(1)} %broadcast_select_fusion.1), channel_id=1, source_target_pairs={{0,32},{32,64},{64,96},{96,128},{128,160},{160,192},{192,224},{224... | collective-permute-start | bytes 983048 | tf_op jit(solution)/shard_map/ppermute | solution.py:21
  90.4 10.7 %collective-permute-done.3 = bf16[1,5,64,512]{3,2,1,0:T(8,128)(2,1)S(1)} collective-permute-done((bf16[1,5,64,512]{3,2,1,0:T(8,128)(2,1)S(1)}, bf16[1,5,64,512]{3,2,1,0:T(8,128)(2,1)S(1)}, u32[]{:S(2)}, u32[]{:S(2)}) %collective-permute-start.3) | collective-permute-done | bytes 327712 | tf_op jit(solution)/shard_map/ppermute | solution.py:21
  101.0 0.1 broadcast_select_fusion
  101.1 0.1 maximum_maximum_fusion
  101.2 1.0 fusion.9
  102.3 1.0 slice_dynamic-update-slice_fusion.2
  103.2 1.0 fusion.10
  104.2 1.0 fusion.11
  105.3 0.9 slice_dynamic-update-slice_fusion.1
  106.2 1.0 fusion.12
  107.2 1.0 fusion.13
  108.2 0.9 slice_dynamic-update-slice_fusion
  109.1 1.0 fusion.14
  110.1 0.0 all-gather.2.cloned.1.call-done
  110.1 10.7 %fusion.25 = (bf16[1,512,3,3,512]{4,1,3,2,0:T(8,128)(2,1)}, bf16[1,512,3,3,512]{4,1,3,2,0:T(8,128)(2,1)}, bf16[1,512,3,3,512]{4,1,3,2,0:T(8,128)(2,1)}) fusion(bf16[3,512,3,3,512]{4,1,3,2,0:T(8,128)(2,1)} %all-gather.2.cloned.1.call-done), kind=kLoop, calls=%fused_computation.46 | loop fusion | bytes 28311552 | tf_op jit(solution)/shard_map/slice | solution.py:56
  120.8 6.7 %copy.27 = bf16[1,512,3,3,512]{1,4,3,2,0:T(8,128)(2,1)} copy(bf16[1,512,3,3,512]{4,1,3,2,0:T(8,128)(2,1)} %get-tuple-element.17) | data formatting | bytes 9437184
  127.5 6.7 %copy.26 = bf16[1,512,3,3,512]{1,4,3,2,0:T(8,128)(2,1)} copy(bf16[1,512,3,3,512]{4,1,3,2,0:T(8,128)(2,1)} %get-tuple-element.16) | data formatting | bytes 9437184
  134.1 0.0 slice-start
  134.1 0.0 slice-start.1
  134.1 4.1 %fusion = f32[3,64,512]{2,1,0:T(8,128)S(1)} fusion(bf16[512,4608,1]{0,1,2:T(8,128)(2,1)} %bitcast.42, bf16[3,3,64,4608]{3,2,1,0:T(8,128)(2,1)} %fusion.14), kind=kOutput, calls=%fused_computation.1 | convolution fusion | flops 905969664 | bytes 6881280 | tf_op jit(solution)/shard_map/fhwc,kc->fhwk/dot_general | solution.py:59
  138.2 0.0 slice-done
  138.2 0.1 slice-done.1
  138.3 2.5 %fusion.1 = f32[3,64,512]{2,1,0:T(8,128)S(1)} fusion(bf16[512,4608,1]{0,1,2:T(8,128)(2,1)S(1)} %bitcast.45, bf16[3,3,64,4608]{3,2,1,0:T(8,128)(2,1)} %fusion.14), kind=kOutput, calls=%fused_computation.3 | convolution fusion | flops 905969664 | bytes 6881280 | tf_op jit(solution)/shard_map/fhwc,kc->fhwk/dot_general | solution.py:59
  140.9 0.0 copy-start
  140.9 0.0 copy-start.1
  140.9 6.7 %copy.25 = bf16[1,512,3,3,512]{1,4,3,2,0:T(8,128)(2,1)} copy(bf16[1,512,3,3,512]{4,1,3,2,0:T(8,128)(2,1)} %get-tuple-element.15) | data formatting | bytes 9437184
  147.6 0.0 copy-done
  147.6 0.0 copy-done.1
  147.6 4.7 %fusion.8 = bf16[1,3,64,512]{3,2,1,0:T(8,128)(2,1)} fusion(f32[3,64,512]{2,1,0:T(8,128)S(1)} %fusion, f32[3,64,512]{2,1,0:T(8,128)S(1)} %fusion.1, bf16[512,4608,1]{0,1,2:T(8,128)(2,1)} %bitcast.41, bf16[3,3,64,4608]{3,2,1,0:T(8,128)(2,1)} %fusion.14, bf16[1,3,64,512]{3,2,1,0:T(8,128)(2,1)S(1)} %copy-done, f32[512]{0:T(512)S(1)} %copy-done.1), kind=kOutput, calls=%fused_computation.11 | convolution fusion | flops 906559488 | bytes 7669760 | tf_op jit(solution)/shard_map/fhwc,kc->fhwk/dot_general | solution.py:55
  (5 shorter events, 0.1 us)
Async XLA Ops:
  6.5 103.6 %all-gather.2.cloned.1.call-start = ((), (), s32[]{:S(2)}) async-start(), calls=%async_computation | async-start | bytes 15040512 | tf_op jit(solution)/shard_map/all_gather | solution.py:101
  61.6 5.4 %collective-permute-start.1 = (bf16[1,1,64,512]{3,2,1,0:T(8,128)(2,1)S(1)}, bf16[1,1,64,512]{3,2,1,0:T(8,128)(2,1)S(1)}, u32[]{:S(2)}, u32[]{:S(2)}) collective-permute-start(bf16[1,1,64,512]{3,2,1,0:T(8,128)(2,1)S(1)} %get-tuple-element.19), channel_id=1, source_target_pairs={{1,0},{2,1},{3,2},{4,3},{5,4},{6,5},{7,6},{8,7},{9,8},{10,9},{11,1... | collective-permute-start | bytes 196616 | tf_op jit(solution)/shard_map/ppermute | solution.py:36
  62.9 5.3 %collective-permute-start = (bf16[1,1,64,512]{3,2,1,0:T(8,128)(2,1)S(1)}, bf16[1,1,64,512]{3,2,1,0:T(8,128)(2,1)S(1)}, u32[]{:S(2)}, u32[]{:S(2)}) collective-permute-start(bf16[1,1,64,512]{3,2,1,0:T(8,128)(2,1)S(1)} %get-tuple-element.18), channel_id=1, source_target_pairs={{0,1},{1,2},{2,3},{3,4},{4,5},{5,6},{6,7},{7,8},{8,9},{9,10},{10,1... | collective-permute-start | bytes 196616 | tf_op jit(solution)/shard_map/ppermute | solution.py:35
  68.3 17.6 %collective-permute-start.2 = (bf16[1,5,64,512]{3,2,1,0:T(8,128)(2,1)S(1)}, bf16[1,5,64,512]{3,2,1,0:T(8,128)(2,1)S(1)}, u32[]{:S(2)}, u32[]{:S(2)}) collective-permute-start(bf16[1,5,64,512]{3,2,1,0:T(8,128)(2,1)S(1)} %pad_maximum_fusion), channel_id=1, source_target_pairs={{0,32},{32,64},{64,96},{96,128},{128,160},{160,192},{192,224},{224... | collective-permute-start | bytes 983048 | tf_op jit(solution)/shard_map/ppermute | solution.py:21
  86.0 15.1 %collective-permute-start.3 = (bf16[1,5,64,512]{3,2,1,0:T(8,128)(2,1)S(1)}, bf16[1,5,64,512]{3,2,1,0:T(8,128)(2,1)S(1)}, u32[]{:S(2)}, u32[]{:S(2)}) collective-permute-start(bf16[1,5,64,512]{3,2,1,0:T(8,128)(2,1)S(1)} %broadcast_select_fusion.1), channel_id=1, source_target_pairs={{0,32},{32,64},{64,96},{96,128},{128,160},{160,192},{192,224},{224... | collective-permute-start | bytes 983048 | tf_op jit(solution)/shard_map/ppermute | solution.py:21
  134.1 4.1 %slice-start = ((s8[4718592]{0:T(1024)(128)(4,1)}), s8[4194304]{0:T(1024)(128)(4,1)S(1)}, s32[]{:S(2)}) async-start(s8[4718592]{0:T(1024)(128)(4,1)} %bitcast.43), calls=%async_computation.1 | async-start | bytes 8388608
  134.1 4.2 %slice-start.1 = ((s8[4718592]{0:T(1024)(128)(4,1)}), s8[524288]{0:T(1024)(128)(4,1)S(1)}, s32[]{:S(2)}) async-start(s8[4718592]{0:T(1024)(128)(4,1)} %bitcast.43), calls=%async_computation.2 | async-start | bytes 1048576
  140.9 6.7 %copy-start = (bf16[1,3,64,512]{3,2,1,0:T(8,128)(2,1)S(1)}, bf16[1,3,64,512]{3,2,1,0:T(8,128)(2,1)}, u32[]{:S(2)}) copy-start(bf16[1,3,64,512]{3,2,1,0:T(8,128)(2,1)} %param.5) | copy-start | bytes 589828
  140.9 6.7 %copy-start.1 = (f32[512]{0:T(512)S(1)}, f32[512]{0:T(512)}, u32[]{:S(2)}) copy-start(f32[512]{0:T(512)} %param.9) | copy-start | bytes 6148
Sparse Core Ops, SparseCore 0:
  9.5 91.1 all-gather.1
where the time goes:
time: 161 us; the launch traced here: 159 us
  blocking collectives  51.5 us (32%)
  local copies, waits for them, and re-layouts  40.2 us (25%)
  waiting for transfers between devices  23.9 us (15%)
  starting transfers between devices  16.2 us (10%)
  between operations  13.5 us (8%)
  matrix products  11.3 us (7%)
  other arithmetic  2.6 us (2%)
    psum x4, blocking collectives, one_axis_at_a_time(): return functools.reduce(lax.psum, axes, x)  51.5 us
    unnamed x19, local copies, waits for them, and re-layouts  28 us
    ppermute x2, waiting for transfers between devices, shifted(): return lax.ppermute(x, axis, pairs)  21.8 us
    ppermute x2, starting transfers between devices, shifted(): return lax.ppermute(x, axis, pairs)  10.9 us
    slice x1, local copies, waits for them, and re-layouts, apply_taps(): flat[0]  10.7 us
    dot_general x2, matrix products, apply_taps(): jnp.einsum('fhwc,kc->fhwk', columns[tap_time:tap_time + frames], flat[tap...  6.64 us
    dot_general x1, matrix products, apply_taps(): jnp.einsum('fhwc,kc->fhwk', columns[0:frames], flat[0], preferred_element...  4.67 us
    ppermute x1, starting transfers between devices, extended_2(): before = lax.ppermute(last, axis, up)  3.99 us
  transfers between devices with their start and end apart: 5, of which 4 were waited for; matrix products, arithmetic and copies ran while one was open for 8% of the time, Pallas kernels for 0%

commit v1 on v0

v1 whole, which is shorter than its diff:
```python
import functools

import jax
import jax.numpy as jnp
from jax import lax
from jax.experimental import pallas as pl
from jax.experimental.pallas import tpu as pltpu
from jax.sharding import Mesh
from jax.sharding import PartitionSpec as P

GROUPS = 32
EPSILON = 1e-06
TM = ("tm_0", "tm_1")
ROWS = ("rows_0", "rows_1")
HIGHEST = lax.Precision.HIGHEST
MESH = pl.DeviceIdType.MESH
LANES = 128
ORDER = (0, 2, 1)


def conv_kernel(
    sizes, feat, gamma, beta, kern, bias, out,
    frames, taps, unfolded, acc, arrived, ready, result, consts, stat_y, stat_z, stat_x,
    affine, local_sem, tap_send, tap_recv, ring_send, ring_recv, halo_send, halo_recv,
    y_send, y_recv, z_send, z_recv, x_send, x_recv, part_send, part_recv, back_send, back_recv,
):
    ny, nz, nx = sizes
    tms = 2 * ny
    half = ny // 2
    rows, width, channels = feat.shape[1:]
    outs = kern.shape[2] // 3
    group = channels // GROUPS
    wide = (rows + 1) * width
    last = rows - 1

    y, core = lax.axis_index("tm_0"), lax.axis_index("tm_1")
    z, x = lax.axis_index("rows_0"), lax.axis_index("rows_1")
    me = 2 * y + core
    row = z * nx + x
    has_up, has_down = row > 0, row < nz * nx - 1
    up = {
        "rows_0": jnp.where(x > 0, z, lax.rem(z + nz - 1, nz)),
        "rows_1": jnp.where(x > 0, x - 1, nx - 1),
    }
    down = {
        "rows_0": jnp.where(x < nx - 1, z, lax.rem(z + 1, nz)),
        "rows_1": jnp.where(x < nx - 1, x + 1, 0),
    }
    y_next, y_prev = lax.rem(y + 1, ny), lax.rem(y + ny - 1, ny)
    partner = {"tm_1": 1 - core}

    def chip(offset):
        return lax.rem(y + ny + offset, ny)

    def remote(src, dst, send, recv, device):
        return pltpu.make_async_remote_copy(
            src_ref=src, dst_ref=dst, send_sem=send, recv_sem=recv,
            device_id=device, device_id_type=MESH,
        )

    own = pltpu.make_async_copy(feat.at[0], frames.at[y, pl.ds(1, rows)], local_sem.at[0])
    own.start()
    small = [
        pltpu.make_async_copy(ref, consts.at[i], local_sem.at[1 + i])
        for i, ref in enumerate((gamma, beta, bias))
    ]
    for copy in small:
        copy.start()
    block = 3 * outs

    def tap_copy(a, b):
        return pltpu.make_async_copy(
            kern.at[a, b],
            taps.at[pl.ds(pl.multiple_of(core * 3 * block + a * block, 16), block), pl.ds(b * channels, channels)],
            local_sem.at[4 + 3 * a + b],
        )

    for a in range(3):
        for b in range(3):
            tap_copy(a, b).start()

    barrier = pltpu.get_barrier_semaphore()

    def tm_peer(k):
        peer = lax.rem(me + k, tms)
        return {"tm_0": peer // 2, "tm_1": lax.rem(peer, 2)}

    def z_peer(k):
        return {"rows_0": lax.rem(z + k, nz)}

    def x_peer(k):
        return {"rows_1": lax.rem(x + k, nx)}

    def each(count, peer, do):
        if count > 1:

            @pl.loop(1, count)
            def _(k):
                do(peer(k))

    def greet(device):
        pl.semaphore_signal(barrier, inc=1, device_id=device, device_id_type=MESH)

    each(tms, tm_peer, greet)
    each(nz, z_peer, greet)
    each(nx, x_peer, greet)
    crosses_up = jnp.logical_and(has_up, x == 0)
    crosses_down = jnp.logical_and(has_down, x == nx - 1)
    if nx > 1:

        @pl.when(crosses_up)
        def _():
            greet(up)

        @pl.when(crosses_down)
        def _():
            greet(down)

    lane = lax.broadcasted_iota(jnp.int32, (channels, LANES), 1)
    chan = lax.broadcasted_iota(jnp.int32, (channels, LANES), 0)
    member = jnp.where(chan // group == lane, 1.0, 0.0)

    def gather_groups(v):
        return lax.dot_general(v, member, (((1,), (0,)), ((), ())), precision=HIGHEST, preferred_element_type=jnp.float32)

    def spread_groups(v):
        return lax.dot_general(v, member, (((1,), (1,)), ((), ())), precision=HIGHEST, preferred_element_type=jnp.float32)

    own.wait()
    count = rows * width
    values = frames[y, 1 : 1 + rows].reshape(count, channels).astype(jnp.float32)
    mean_c = jnp.sum(values, axis=0, keepdims=True) * (1.0 / count)
    off = values - mean_c
    m2_c = jnp.sum(off * off, axis=0, keepdims=True)
    mean_c8 = jnp.broadcast_to(mean_c, (8, channels))
    mean_g = gather_groups(mean_c8) * (1.0 / group)
    apart = mean_c8 - spread_groups(mean_g)
    m2_g = gather_groups(m2_c + count * (apart * apart))
    stat_y[me] = jnp.concatenate([mean_g[0:1], m2_g[0:1]], axis=0)

    acc[...] = jnp.zeros_like(acc)
    unfolded[rows * width :, :] = jnp.zeros((width, 3 * channels), unfolded.dtype)

    expected = tms - 1 + nz - 1 + nx - 1
    if nx > 1:
        expected = expected + jnp.where(crosses_up, 1, 0) + jnp.where(crosses_down, 1, 0)
    pl.semaphore_wait(barrier, expected)

    def publish(buf, mine, count, peer, send, recv):
        if count > 1:

            @pl.loop(1, count)
            def _(k):
                remote(buf.at[mine], buf.at[mine], send.at[k], recv.at[mine], peer(k)).start()

    def collect(buf, mine, count, send, recv, weight):
        if count > 1:

            @pl.loop(1, count)
            def _(k):
                other = lax.rem(mine + k, count)
                remote(buf.at[other], buf.at[other], send.at[k], recv.at[other], {"tm_0": y_next}).wait_recv()

        means, m2s = buf[:, 0:1, :], buf[:, 1:2, :]
        mean = jnp.sum(means, axis=0) * (1.0 / count)
        gap = means - mean[None]
        m2 = jnp.sum(m2s, axis=0) + weight * jnp.sum(gap * gap, axis=0)
        return jnp.concatenate([mean, m2], axis=0)

    publish(stat_y, me, tms, tm_peer, y_send, y_recv)

    def ring_copy(src, way, chunk):
        at = frames.at[src, 1 + chunk]
        return remote(at, at, ring_send.at[src, way, chunk], ring_recv.at[src, chunk], {"tm_0": y_next if way == 0 else y_prev})

    def halo_copy(src, side):
        at, to = (1, rows + 1) if side == 0 else (rows, 0)
        return remote(
            frames.at[src, at], frames.at[src, to], halo_send.at[src, side], halo_recv.at[src, side], up if side == 0 else down,
        )

    def send_halo(src, chunk):
        if chunk == 0:
            pl.when(has_up)(lambda: halo_copy(src, 0).start())
        if chunk == last:
            pl.when(has_down)(lambda: halo_copy(src, 1).start())

    for chunk in ORDER:
        ring_copy(y, 0, chunk).start()
        ring_copy(y, 1, chunk).start()
    for chunk in (0, last):
        send_halo(y, chunk)

    def tap_remote():
        at = taps.at[pl.ds(pl.multiple_of(core * 3 * block, 16), 3 * block)]
        return remote(at, at, tap_send, tap_recv, partner)

    for a in range(3):
        for b in range(3):
            tap_copy(a, b).wait()
    tap_remote().start()

    def ring_event(step, chunk):
        for way in (0, 1):
            src = chip(-step) if way == 0 else chip(step)

            def arrive(src=src, way=way):
                ring_copy(src, way, chunk).wait_recv()
                if step < half - 1:
                    ring_copy(src, way, chunk).start()
                elif step == half - 1:
                    pl.when(core == way)(lambda: ring_copy(src, way, chunk).start())
                send_halo(src, chunk)

            if step < half:
                arrive()
            else:
                pl.when(core == way)(arrive)

    for copy in small:
        copy.wait()
    per_device = float(rows * width * group)
    for chunk in ORDER:
        if half > 2 and chunk == ORDER[0]:
            pass
    stat_z[z] = collect(stat_y, me, tms, y_send, y_recv, per_device)
    publish(stat_z, z, nz, z_peer, z_send, z_recv)
    pre = [(step, chunk) for step in range(1, half - 1) for chunk in ORDER]
    cut = len(pre) * 2 // 3
    for step, chunk in pre[:cut]:
        ring_event(step, chunk)
    stat_x[x] = collect(stat_z, z, nz, z_send, z_recv, per_device * tms)
    publish(stat_x, x, nx, x_peer, x_send, x_recv)
    for step, chunk in pre[cut:]:
        ring_event(step, chunk)
    final = collect(stat_x, x, nx, x_send, x_recv, per_device * tms * nz)
    total = per_device * tms * nz * nx
    inv = lax.rsqrt(final[1:2] * (1.0 / total) + EPSILON)
    both = spread_groups(jnp.concatenate([final[0:1], inv] + [jnp.zeros((6, LANES), jnp.float32)], axis=0))
    affine[0:1] = both[0:1]
    affine[1:2] = 0.5 * both[1:2] * consts[0]
    affine[2:3] = 0.5 * consts[1]
    tap_remote().wait_recv()

    column = lax.rem(lax.broadcasted_iota(jnp.int32, (outs, wide), 1), width)
    at_left, at_right = column == 0, column == width - 1

    def process(src):
        for r in (1, rows, 0, rows + 1, *range(2, rows)):
            if r == 0:
                pl.when(has_up)(lambda: halo_copy(src, 1).wait_recv())
            if r == rows + 1:
                pl.when(has_down)(lambda: halo_copy(src, 0).wait_recv())
            value = frames[src, r].astype(jnp.float32)
            h = (value - affine[0:1]) * affine[1:2] + affine[2:3]
            active = h + h * jnp.tanh(h)
            if r == 0:
                active = jnp.where(has_up, active, 0.0)
            if r == rows + 1:
                active = jnp.where(has_down, active, 0.0)
            active = active.astype(unfolded.dtype)
            for b in range(3):
                if 0 <= r - b < rows:
                    unfolded[(r - b) * width : (r - b + 1) * width, b * channels : (b + 1) * channels] = active
        product = lax.dot_general(
            taps[...], unfolded[...], (((1,), (1,)), ((), ())), preferred_element_type=jnp.float32
        )
        frame = 2 * src + core

        for owner in (0, 1):
            for a in range(3):
                base = (owner * 3 + a) * block
                one, two, three = (product[base + c * outs : base + (c + 1) * outs] for c in range(3))
                one = jnp.where(at_left, 0.0, pltpu.roll(one, 1, 1))
                three = jnp.where(at_right, 0.0, pltpu.roll(three, wide - 1, 1))
                total = one + two + three
                acc[owner, frame + 2 - a] += total
                if a < 2:

                    @pl.when(frame == 0)
                    def _():
                        acc[owner, 0] += total
                        if a == 0:
                            acc[owner, 1] += total

    def released(j):
        return chip((j + 1) // 2) if j % 2 else chip(1 - j // 2)

    def part_copy(to):
        return remote(acc.at[1 - core, pl.ds(2 * to, 2)], arrived.at[to], part_send.at[to], part_recv.at[to], partner)

    def back_copy(to, which):
        return remote(
            ready.at[to, which], result.at[me], back_send.at[to, which], back_recv.at[me], {"tm_0": to, "tm_1": which}
        )

    def finish(to):
        part_copy(to).wait_recv()
        for which in (0, 1):
            value = (acc[core, 2 * to + which] + arrived[to, which]).astype(ready.dtype)
            mine = jnp.logical_and(to == y, core == which)

            @pl.when(mine)
            def _():
                result[me] = value

            @pl.when(jnp.logical_not(mine))
            def _():
                ready[to, which] = value
                back_copy(to, which).start()

    def released_at(j):
        return jnp.where(lax.rem(j, 2) == 1, chip((j + 1) // 2), chip(1 - j // 2))

    events = {}
    if half > 1:
        for n, chunk in enumerate(ORDER):
            events.setdefault(min(n, ny - 3), []).append((half - 1, chunk))
    for n, chunk in enumerate(ORDER):
        events.setdefault(ny - 3 + n, []).append((half, chunk))

    @pl.loop(0, ny)
    def _(i):
        for when, todo in events.items():

            @pl.when(i == when)
            def _():
                for step, chunk in todo:
                    ring_event(step, chunk)

        src = chip(jnp.where(lax.rem(i, 2) == 1, (i + 1) // 2, -(i // 2)))
        process(src)

        @pl.when(i > 0)
        def _():
            part_copy(released_at(i)).start()

        @pl.when(i > 1)
        def _():
            finish(released_at(i - 1))

    part_copy(released(ny)).start()
    finish(released(ny - 1))
    finish(released(ny))

    @pl.loop(1, tms)
    def _(k):
        other = lax.rem(me + k, tms)
        remote(result.at[other], result.at[other], back_send.at[0, 0], back_recv.at[other], partner).wait_recv()

    conv = result[...].reshape(channels, wide).astype(jnp.float32)
    conv = jnp.transpose(conv, (1, 0))[: rows * width]
    kept = frames[y, 1 : 1 + rows].reshape(rows * width, channels).astype(jnp.float32)
    total = kept + conv + consts[2]
    out[...] = total.astype(out.dtype).reshape(out.shape)

    def drain(buf, mine, count, send, recv):
        if count > 1:

            @pl.loop(1, count)
            def _(k):
                remote(buf.at[mine], buf.at[mine], send.at[k], recv.at[mine], partner).wait_send()

    drain(stat_y, me, tms, y_send, y_recv)
    drain(stat_z, z, nz, z_send, z_recv)
    drain(stat_x, x, nx, x_send, x_recv)
    tap_remote().wait_send()

    @pl.loop(0, rows)
    def _(chunk):
        for way in (0, 1):
            for step in range(half):
                src = chip(-step) if way == 0 else chip(step)

                def sent(src=src, way=way):
                    ring_copy(src, way, chunk).wait_send()

                if step < half - 1:
                    sent()
                else:
                    pl.when(core == way)(sent)

    @pl.loop(0, ny)
    def _(src):
        pl.when(has_up)(lambda: halo_copy(src, 0).wait_send())
        pl.when(has_down)(lambda: halo_copy(src, 1).wait_send())
        part_copy(src).wait_send()
        for which in (0, 1):

            @pl.when(jnp.logical_not(jnp.logical_and(src == y, core == which)))
            def _():
                back_copy(src, which).wait_send()


def local(sizes, features, gamma, beta, kernel, bias):
    ny, nz, nx = sizes
    tms = 2 * ny
    _, rows, width, channels = features.shape
    outs = kernel.shape[1]
    taps = jnp.transpose(kernel, (0, 2, 3, 1, 4)).reshape(3, 3, 3 * outs, channels)
    wide = (rows + 1) * width
    bf16, f32 = jnp.bfloat16, jnp.float32
    dma = pltpu.SemaphoreType.DMA
    any_spec = pl.BlockSpec(memory_space=pl.ANY)
    vector = lambda v: v.reshape(1, channels)
    return pl.pallas_call(
        functools.partial(conv_kernel, sizes),
        out_shape=jax.ShapeDtypeStruct(features.shape, bf16),
        in_specs=[any_spec] * 5,
        out_specs=pl.BlockSpec(memory_space=pltpu.VMEM),
        scratch_shapes=[
            pltpu.VMEM((ny, rows + 2, width, channels), bf16),
            pltpu.VMEM((18 * outs, 3 * channels), bf16),
            pltpu.VMEM((wide, 3 * channels), bf16),
            pltpu.VMEM((2, tms + 2, outs, wide), f32),
            pltpu.VMEM((ny, 2, outs, wide), f32),
            pltpu.VMEM((ny, 2, outs, wide), bf16),
            pltpu.VMEM((tms, outs, wide), bf16),
            pltpu.VMEM((3, 1, channels), f32),
            pltpu.VMEM((tms, 2, LANES), f32),
            pltpu.VMEM((nz, 2, LANES), f32),
            pltpu.VMEM((nx, 2, LANES), f32),
            pltpu.VMEM((8, channels), f32),
            dma((13,)),
            dma, dma,
            dma((ny, 2, rows)), dma((ny, rows)),
            dma((ny, 2)), dma((ny, 2)),
            dma((tms,)), dma((tms,)),
            dma((nz,)), dma((nz,)),
            dma((nx,)), dma((nx,)),
            dma((ny,)), dma((ny,)),
            dma((ny, 2)), dma((tms,)),
        ],
        compiler_params=pltpu.CompilerParams(collective_id=0, has_side_effects=True, vmem_limit_bytes=60 << 20),
        name="fused_block",
    )(features, vector(gamma), vector(beta), taps, vector(bias))


def solution(mesh):
    sizes = (8, 8, 4)
    split = Mesh(mesh.devices.reshape(8, 2, 8, 4), TM + ROWS)
    in_specs = (P(TM, ROWS, None, None), P(), P(), P(None, TM, None, None, None), P())
    out_specs = P(TM, ROWS, None, None)
    return jax.shard_map(
        functools.partial(local, sizes), mesh=split, in_specs=in_specs, out_specs=out_specs, check_vma=False
    )
```

time: 161 us -> 51.9 us (0.32)
  the two profiles are of different devices: /device:TPU:1 before, /device:TPU:11 now
where the time goes in v1:
time: 51.9 us; the launch traced here: 51.7 us
  Pallas kernels  50.1 us (97%)
  local copies, waits for them, and re-layouts  1.62 us (3%)
    pallas_call x1, Pallas kernels, local(): pl.pallas_call(functools.partial(conv_kernel, sizes), out_shape=jax.Shape...  50.1 us
    unnamed x1, local copies, waits for them, and re-layouts  1.62 us

profile of v1, /device:TPU:11, one launch (start us, length us, event | category | flops | bytes accessed | tf_op | source)
XLA Modules:
  0.0 51.7 jit_solution(9311643132440235984)
XLA Ops:
  0.0 50.1 %fused_block.1 = bf16[1,3,64,512]{3,2,1,0:T(8,128)(2,1)} custom-call(bf16[1,3,64,512]{3,2,1,0:T(8,128)(2,1)} %feat.1, f32[1,512]{1,0:T(1,128)} %bitcast.7, f32[1,512]{1,0:T(1,128)} %bitcast.8, bf16[3,3,96,512]{3,2,1,0:T(8,128)(2,1)} %bitcast.6, f32[1,512]{1,0:T(1,128)} %bitcast.9), custom_call_target="tpu_custom_call" | custom-call | tf_op jit(solution)/shard_map/fused_block/pallas_call | solution.py:406
  50.1 1.6 %copy.7 = bf16[1,3,64,512]{3,2,1,0:T(8,128)(2,1)} copy(bf16[1,3,64,512]{3,2,1,0:T(8,128)(2,1)} %fused_block.1) | data formatting | bytes 393216

commit v2 on v1

v2 whole, which is shorter than its diff:
```python
import functools

import jax
import jax.numpy as jnp
from jax import lax
from jax.experimental import pallas as pl
from jax.experimental.pallas import tpu as pltpu
from jax.sharding import Mesh
from jax.sharding import PartitionSpec as P

GROUPS = 32
EPSILON = 1e-06
TM = ("tm_0", "tm_1")
ROWS = ("rows_0", "rows_1")
HIGHEST = lax.Precision.HIGHEST
MESH = pl.DeviceIdType.MESH
LANES = 128
VMEM_LIMIT = 67043328 - 409600
ORDER = (0, 2, 1)


def conv_kernel(
    sizes, feat, gamma, beta, kern, out,
    frames, taps, wide_a, wide_b, acc, arrived, ready, result, consts, stat_y, stat_z, stat_x,
    affine, local_sem, tap_sem, ring_send, ring_recv, halo_send, halo_recv,
    y_sem, z_sem, x_sem, part_send, part_recv, back_sem,
):
    ny, nz, nx = sizes
    tms = 2 * ny
    half = ny // 2
    rows, width, channels = feat.shape[1:]
    outs = kern.shape[2] // 3
    group = channels // GROUPS
    wide = (rows + 1) * width
    last = rows - 1
    slot = rows + 2

    y, core = lax.axis_index("tm_0"), lax.axis_index("tm_1")
    z, x = lax.axis_index("rows_0"), lax.axis_index("rows_1")
    me = 2 * y + core
    row = z * nx + x
    has_up, has_down = row > 0, row < nz * nx - 1
    inner = jnp.logical_and(has_up, has_down)

    def wrap(v, n):
        v = jnp.where(v >= n, v - n, v)
        return jnp.where(v < 0, v + n, v)

    def chip(offset):
        return wrap(y + offset, ny)

    up = {"rows_0": jnp.where(x > 0, z, wrap(z - 1, nz)), "rows_1": jnp.where(x > 0, x - 1, nx - 1)}
    down = {"rows_0": jnp.where(x < nx - 1, z, wrap(z + 1, nz)), "rows_1": jnp.where(x < nx - 1, x + 1, 0)}
    y_next, y_prev = chip(1), chip(-1)
    partner = {"tm_1": 1 - core}
    home = y * slot

    def remote(src, dst, send, recv, device):
        return pltpu.make_async_remote_copy(
            src_ref=src, dst_ref=dst, send_sem=send, recv_sem=recv,
            device_id=device, device_id_type=MESH,
        )

    own = pltpu.make_async_copy(feat.at[0], frames.at[pl.ds(home + 1, rows)], local_sem.at[0])
    own.start()

    barrier = pltpu.get_barrier_semaphore()

    def far_first(n):
        return sorted(range(1, n), key=lambda k: -min(k, n - k))

    y_peers = [{"tm_0": chip(k), "tm_1": c} for k in far_first(ny) for c in (core, 1 - core)] + [partner]
    z_peers = [{"rows_0": wrap(z + k, nz)} for k in far_first(nz)]
    x_peers = [{"rows_1": wrap(x + k, nx)} for k in far_first(nx)]

    def greet(device):
        pl.semaphore_signal(barrier, inc=1, device_id=device, device_id_type=MESH)

    for peer in y_peers + z_peers + x_peers:
        greet(peer)
    crosses_up = jnp.logical_and(has_up, x == 0)
    crosses_down = jnp.logical_and(has_down, x == nx - 1)
    expected = len(y_peers) + len(z_peers) + len(x_peers)
    if nx > 1:
        pl.when(crosses_up)(lambda: greet(up))
        pl.when(crosses_down)(lambda: greet(down))
        expected = expected + jnp.where(crosses_up, 1, 0) + jnp.where(crosses_down, 1, 0)

    for i, ref in enumerate((gamma, beta)):
        pltpu.make_async_copy(ref, consts.at[i], local_sem.at[1]).start()
    block = 3 * outs
    mine = pl.ds(pl.multiple_of(core * 3 * block, 16), 3 * block)
    for a in range(3):
        for b in range(3):
            pltpu.make_async_copy(
                kern.at[a, b],
                taps.at[pl.ds(pl.multiple_of(core * 3 * block + a * block, 16), block), pl.ds(b * channels, channels)],
                local_sem.at[2],
            ).start()

    lane = lax.broadcasted_iota(jnp.int32, (channels, LANES), 1)
    chan = lax.broadcasted_iota(jnp.int32, (channels, LANES), 0)
    member = jnp.where(chan // group == lane, 1.0, 0.0)

    def gather_groups(v):
        return lax.dot_general(v, member, (((1,), (0,)), ((), ())), precision=HIGHEST, preferred_element_type=jnp.float32)

    def spread_groups(v):
        return lax.dot_general(v, member, (((1,), (1,)), ((), ())), precision=HIGHEST, preferred_element_type=jnp.float32)

    acc[...] = jnp.zeros_like(acc)
    for unfolded in (wide_a, wide_b):
        unfolded[rows * width :, :] = jnp.zeros((width, 3 * channels), unfolded.dtype)

    own.wait()
    count = rows * width
    values = frames[pl.ds(home + 1, rows)].reshape(count, channels).astype(jnp.float32)
    mean_c = jnp.sum(values, axis=0, keepdims=True) * (1.0 / count)
    off = values - mean_c
    m2_c = jnp.sum(off * off, axis=0, keepdims=True)
    mean_c8 = jnp.broadcast_to(mean_c, (8, channels))
    mean_g = gather_groups(mean_c8) * (1.0 / group)
    apart = mean_c8 - spread_groups(mean_g)
    m2_g = gather_groups(m2_c + count * (apart * apart))
    stat_y[me] = jnp.concatenate([mean_g[0:1], m2_g[0:1]], axis=0)

    pl.semaphore_wait(barrier, expected)

    def publish(buf, at, peers, sem):
        for peer in peers:
            remote(buf.at[at], buf.at[at], sem.at[0], sem.at[1], peer).start()

    def several(buf, n, sem):
        return remote(buf.at[pl.ds(0, n)], buf.at[pl.ds(0, n)], sem.at[0], sem.at[1], partner)

    def collect(buf, peers, sem, weight):
        if peers:
            several(buf, len(peers), sem).wait_recv()
        means, m2s = buf[:, 0:1, :], buf[:, 1:2, :]
        mean = jnp.sum(means, axis=0) * (1.0 / buf.shape[0])
        gap = means - mean[None]
        m2 = jnp.sum(m2s, axis=0) + weight * jnp.sum(gap * gap, axis=0)
        return jnp.concatenate([mean, m2], axis=0)

    publish(stat_y, me, y_peers, y_sem)

    def ring_copy(src, way, chunk):
        at = frames.at[src * slot + 1 + chunk]
        return remote(at, at, ring_send, ring_recv.at[src, chunk], {"tm_0": y_next if way == 0 else y_prev})

    def halo_copy(src, side):
        at, to = (1, rows + 1) if side == 0 else (rows, 0)
        return remote(
            frames.at[src * slot + at], frames.at[src * slot + to], halo_send, halo_recv.at[src], up if side == 0 else down
        )

    def send_halo(src, chunk):
        if chunk == 0:
            pl.when(has_up)(lambda: halo_copy(src, 0).start())
        if chunk == last:
            pl.when(has_down)(lambda: halo_copy(src, 1).start())

    for chunk in ORDER:
        ring_copy(y, 0, chunk).start()
        ring_copy(y, 1, chunk).start()
    for chunk in (0, last):
        send_halo(y, chunk)

    pltpu.make_async_copy(taps.at[mine], taps.at[mine], local_sem.at[2]).wait()
    tap_remote = remote(taps.at[mine], taps.at[mine], tap_sem.at[0], tap_sem.at[1], partner)
    tap_remote.start()
    pltpu.make_async_copy(consts, consts, local_sem.at[1]).wait()

    def ring_event(step, chunk):
        for way in (0, 1):
            src = chip(-step) if way == 0 else chip(step)

            def arrive(src=src, way=way):
                ring_copy(src, way, chunk).wait_recv()
                if step < half - 1:
                    ring_copy(src, way, chunk).start()
                elif step == half - 1:
                    pl.when(core == way)(lambda: ring_copy(src, way, chunk).start())
                send_halo(src, chunk)

            if step < half:
                arrive()
            else:
                pl.when(core == way)(arrive)

    per_device = float(rows * width * group)
    early = [(step, chunk) for step in range(1, half - 1) for chunk in ORDER]

    def ring_events(todo):
        for step, chunk in todo:
            ring_event(step, chunk)

    ring_events(early[:1])
    stat_z[z] = collect(stat_y, y_peers, y_sem, per_device)
    publish(stat_z, z, z_peers, z_sem)
    ring_events(early[1:4])
    stat_x[x] = collect(stat_z, z_peers, z_sem, per_device * tms)
    publish(stat_x, x, x_peers, x_sem)
    ring_events(early[4:])
    final = collect(stat_x, x_peers, x_sem, per_device * tms * nz)
    total = per_device * tms * nz * nx
    inv = lax.rsqrt(final[1:2] * (1.0 / total) + EPSILON)
    both = spread_groups(jnp.concatenate([final[0:1], inv] + [jnp.zeros((6, LANES), jnp.float32)], axis=0))
    affine[0:1] = both[0:1]
    affine[1:2] = 0.5 * both[1:2] * consts[0]
    affine[2:3] = 0.5 * consts[1]
    tap_remote.wait_recv()

    column = lax.rem(lax.broadcasted_iota(jnp.int32, (outs, wide), 1), width)
    at_left, at_right = column == 0, column == width - 1

    def source(k):
        if isinstance(k, int):
            return chip((k + 1) // 2 if k % 2 else -(k // 2))
        return chip(jnp.where(lax.rem(k, 2) == 1, (k + 1) // 2, -(k // 2)))

    def halo_wait(src):
        def rows_in(n):
            at = frames.at[pl.ds(0, n)]
            remote(at, at, halo_send, halo_recv.at[src], partner).wait_recv()

        pl.when(inner)(lambda: rows_in(2))
        pl.when(jnp.logical_not(inner))(lambda: rows_in(1))

    def prepare(src, unfolded):
        for r in range(rows + 2):
            value = frames[src * slot + r].astype(jnp.float32)
            h = (value - affine[0:1]) * affine[1:2] + affine[2:3]
            active = h + h * jnp.tanh(h)
            if r == 0:
                active = jnp.where(has_up, active, 0.0)
            if r == rows + 1:
                active = jnp.where(has_down, active, 0.0)
            active = active.astype(unfolded.dtype)
            for b in range(3):
                if 0 <= r - b < rows:
                    unfolded[(r - b) * width : (r - b + 1) * width, b * channels : (b + 1) * channels] = active

    def multiply(src, unfolded):
        frame = 2 * src + core
        totals = []
        for owner in (0, 1):
            product = lax.dot_general(
                taps[owner * 3 * block : (owner + 1) * 3 * block], unfolded[...], (((1,), (1,)), ((), ())),
                preferred_element_type=jnp.float32,
            )
            for a in range(3):
                base = a * block
                one, two, three = (product[base + c * outs : base + (c + 1) * outs] for c in range(3))
                one = jnp.where(at_left, 0.0, pltpu.roll(one, 1, 1))
                three = jnp.where(at_right, 0.0, pltpu.roll(three, wide - 1, 1))
                total = one + two + three
                acc[owner, frame + 2 - a] += total
                totals.append(total)
        return totals

    def repeat_first(src, totals):
        @pl.when(2 * src + core == 0)
        def _():
            for owner in (0, 1):
                acc[owner, 0] += totals[3 * owner] + totals[3 * owner + 1]
                acc[owner, 1] += totals[3 * owner]

    def released(j):
        if isinstance(j, int):
            return chip((j + 1) // 2 if j % 2 else 1 - j // 2)
        return chip(jnp.where(lax.rem(j, 2) == 1, (j + 1) // 2, 1 - j // 2))

    def part_copy(to):
        return remote(acc.at[1 - core, pl.ds(2 * to, 2)], arrived.at[to], part_send, part_recv.at[to], partner)

    low = lax.broadcasted_iota(jnp.int32, (outs // 2, LANES), 1) < width

    def finish(to):
        part_copy(to).wait_recv()
        for which in (0, 1):
            value = acc[core, 2 * to + which] + arrived[to, which]
            rest = value[:, LANES:]
            packed = jnp.where(low, rest[: outs // 2], pltpu.roll(rest[outs // 2 :], width, 1))
            value = jnp.concatenate([value[:, :LANES], packed], axis=0).astype(ready.dtype)
            stays = jnp.logical_and(to == y, core == which)

            @pl.when(stays)
            def _():
                result[me] = value

            @pl.when(jnp.logical_not(stays))
            def _():
                ready[2 * to + which] = value
                remote(ready.at[2 * to + which], result.at[me], back_sem.at[0], back_sem.at[1], {"tm_0": to, "tm_1": which}).start()

    late = [(step, chunk) for step in (half - 1, half) for chunk in ORDER]
    if ny >= 8:
        events = {1: late[:1], 2: late[1:2], ny - 4: late[2:3], ny - 3: late[3:5], ny - 2: late[5:]}
    else:
        events = {1: late[:3], ny - 1: late[3:]}

    def stage(i, current, following):
        if isinstance(i, int):
            ring_events(events.get(i + 1, []))
        else:
            for k, todo in events.items():
                pl.when(i + 1 == k)(functools.partial(ring_events, todo))
        halo_wait(source(i + 1))
        prepare(source(i + 1), following)
        after(i, current)

    def after(i, current):
        src = source(i)
        totals = multiply(src, current)
        repeat_first(src, totals)
        if isinstance(i, int):
            if i > 0:
                part_copy(released(i)).start()
            if i > 1:
                finish(released(i - 1))
        else:
            pl.when(i > 0)(lambda: part_copy(released(i)).start())
            pl.when(i > 1)(lambda: finish(released(i - 1)))

    halo_wait(source(0))
    prepare(source(0), wide_a)

    @pl.loop(0, half - 1)
    def _(p):
        stage(2 * p, wide_a, wide_b)
        stage(2 * p + 1, wide_b, wide_a)

    stage(ny - 2, wide_a, wide_b)
    after(ny - 1, wide_b)
    part_copy(released(ny)).start()
    finish(released(ny - 1))
    finish(released(ny))

    several(result, tms - 1, back_sem).wait_recv()
    conv = jnp.transpose(result[:, :outs].reshape(channels, LANES).astype(jnp.float32), (1, 0))
    out[0, : rows - 1] = conv.astype(out.dtype).reshape(rows - 1, width, channels)
    rest = result[:, outs:].astype(jnp.float32)
    rest = jnp.concatenate([rest, pltpu.roll(rest, width, 2)], axis=1).reshape(channels, LANES)
    rest = jnp.transpose(rest, (1, 0))[:width]
    out[0, last] = rest.astype(out.dtype)

    for buf, n, sem in ((stat_y, tms, y_sem), (stat_z, nz, z_sem), (stat_x, nx, x_sem), (ready, tms, back_sem)):
        if n > 1:
            several(buf, n - 1, sem).wait_send()
    tap_remote.wait_send()

    def rows_out(n, sem):
        at = frames.at[pl.ds(0, n)]
        remote(at, at, sem, halo_recv.at[0], partner).wait_send()

    rows_out(rows * (2 * half - 1), ring_send)
    pl.when(inner)(lambda: rows_out(2 * ny, halo_send))
    pl.when(jnp.logical_not(inner))(lambda: rows_out(ny, halo_send))
    remote(arrived, arrived, part_send, part_recv.at[0], partner).wait_send()


def local(sizes, features, gamma, beta, kernel, bias):
    ny, nz, nx = sizes
    tms = 2 * ny
    _, rows, width, channels = features.shape
    outs = kernel.shape[1]
    taps = jnp.transpose(kernel, (0, 2, 3, 1, 4)).reshape(3, 3, 3 * outs, channels)
    wide = (rows + 1) * width
    bf16, f32 = jnp.bfloat16, jnp.float32
    dma = pltpu.SemaphoreType.DMA
    any_spec = pl.BlockSpec(memory_space=pltpu.HBM)
    vector = lambda v: v.reshape(1, channels)
    conv = pl.pallas_call(
        functools.partial(conv_kernel, sizes),
        out_shape=pltpu.VMEM(features.shape, bf16),
        in_specs=[any_spec] * 4,
        out_specs=pl.BlockSpec(memory_space=pltpu.VMEM),
        scratch_shapes=[
            pltpu.VMEM((ny * (rows + 2), width, channels), bf16),
            pltpu.VMEM((18 * outs, 3 * channels), bf16),
            pltpu.VMEM((wide, 3 * channels), bf16),
            pltpu.VMEM((wide, 3 * channels), bf16),
            pltpu.VMEM((2, tms + 2, outs, wide), f32),
            pltpu.VMEM((ny, 2, outs, wide), f32),
            pltpu.VMEM((tms, outs * 3 // 2, LANES), bf16),
            pltpu.VMEM((tms, outs * 3 // 2, LANES), bf16),
            pltpu.VMEM((2, 1, channels), f32),
            pltpu.VMEM((tms, 2, LANES), f32),
            pltpu.VMEM((nz, 2, LANES), f32),
            pltpu.VMEM((nx, 2, LANES), f32),
            pltpu.VMEM((8, channels), f32),
            dma((3,)), dma((2,)),
            dma, dma((ny, rows)),
            dma, dma((ny,)),
            dma((2,)), dma((2,)), dma((2,)),
            dma, dma((ny,)),
            dma((2,)),
        ],
        compiler_params=pltpu.CompilerParams(collective_id=0, has_side_effects=True, vmem_limit_bytes=VMEM_LIMIT),
        name="fused_block",
    )(features, vector(gamma), vector(beta), taps)
    return (features.astype(f32) + conv.astype(f32) + bias).astype(bf16)


def solution(mesh):
    sizes = (8, 8, 4)
    split = Mesh(mesh.devices.reshape(8, 2, 8, 4), TM + ROWS)
    in_specs = (P(TM, ROWS, None, None), P(), P(), P(None, TM, None, None, None), P())
    out_specs = P(TM, ROWS, None, None)
    return jax.shard_map(
        functools.partial(local, sizes), mesh=split, in_specs=in_specs, out_specs=out_specs, check_vma=False
    )
```

time: 51.9 us -> 46 us (0.89)
  the two profiles are of different devices: /device:TPU:11 before, /device:TPU:1 now
where the time goes in v2:
time: 46 us; the launch traced here: 45.9 us
  Pallas kernels  45.1 us (98%)
  other arithmetic  0.74 us (2%)
    pallas_call x1, Pallas kernels, local(): pl.pallas_call(functools.partial(conv_kernel, sizes), out_shape=pltpu.VME...  45.1 us

profile of v2, /device:TPU:1, one launch (start us, length us, event | category | flops | bytes accessed | tf_op | source)
XLA Modules:
  0.0 45.9 jit_solution(16518017228156021030)
XLA Ops:
  0.0 0.0 copy-start
  0.0 0.0 copy-start.1
  0.0 45.1 %fused_block.1 = bf16[1,3,64,512]{3,2,1,0:T(8,128)(2,1)S(1)} custom-call(bf16[1,3,64,512]{3,2,1,0:T(8,128)(2,1)} %feat.1, f32[1,512]{1,0:T(1,128)} %bitcast.6, f32[1,512]{1,0:T(1,128)} %bitcast.7, bf16[3,3,96,512]{3,2,1,0:T(8,128)(2,1)} %bitcast.5), custom_call_target="tpu_custom_call" | custom-call | tf_op jit(solution)/shard_map/fused_block/pallas_call | solution.py:374
  45.1 0.0 copy-done
  45.2 0.0 copy-done.1
  45.2 0.7 %add_convert_fusion = bf16[1,3,64,512]{3,2,1,0:T(8,128)(2,1)} fusion(bf16[1,3,64,512]{3,2,1,0:T(8,128)(2,1)S(1)} %fused_block.1, bf16[1,3,64,512]{3,2,1,0:T(8,128)(2,1)S(1)} %copy-done, f32[512]{0:T(512)S(1)} %copy-done.1), kind=kLoop, calls=%fused_computation | loop fusion | flops 491520 | bytes 591872 | tf_op jit(solution)/shard_map/convert_element_type | solution.py:403
Async XLA Ops:
  0.0 45.1 %copy-start = (bf16[1,3,64,512]{3,2,1,0:T(8,128)(2,1)S(1)}, bf16[1,3,64,512]{3,2,1,0:T(8,128)(2,1)}, u32[]{:S(2)}) copy-start(bf16[1,3,64,512]{3,2,1,0:T(8,128)(2,1)} %feat.1) | copy-start | bytes 589828
  0.0 45.2 %copy-start.1 = (f32[512]{0:T(512)S(1)}, f32[512]{0:T(512)}, u32[]{:S(2)}) copy-start(f32[512]{0:T(512)} %param.9) | copy-start | bytes 6148

commit v3 on v2

--- a/solution.py
+++ b/solution.py
@@ -21,9 +21,9 @@
 
 def conv_kernel(
     sizes, feat, gamma, beta, kern, out,
-    frames, taps, wide_a, wide_b, acc, arrived, ready, result, consts, stat_y, stat_z, stat_x,
+    frames, taps, wide_a, wide_b, prod_a, prod_b, acc, arrived, ready, result, consts, stat_y, stat_z, stat_x, stat_all,
     affine, local_sem, tap_sem, ring_send, ring_recv, halo_send, halo_recv,
-    y_sem, z_sem, x_sem, part_send, part_recv, back_sem,
+    y_sem, z_sem, x_sem, all_sem, part_send, part_recv, back_sem,
 ):
     ny, nz, nx = sizes
     tms = 2 * ny
@@ -196,13 +196,34 @@
             ring_event(step, chunk)
 
     ring_events(early[:1])
-    stat_z[z] = collect(stat_y, y_peers, y_sem, per_device)
-    publish(stat_z, z, z_peers, z_sem)
+    lead = core == 1
+    span = collect(stat_y, y_peers, y_sem, per_device)
+
+    @pl.when(lead)
+    def _():
+        stat_z[z] = span
+        publish(stat_z, z, z_peers, z_sem)
+
     ring_events(early[1:4])
-    stat_x[x] = collect(stat_z, z_peers, z_sem, per_device * tms)
-    publish(stat_x, x, x_peers, x_sem)
+
+    @pl.when(lead)
+    def _():
+        stat_x[x] = collect(stat_z, z_peers, z_sem, per_device * tms)
+        publish(stat_x, x, x_peers, x_sem)
+
     ring_events(early[4:])
-    final = collect(stat_x, x_peers, x_sem, per_device * tms * nz)
+    hand_over = remote(stat_all, stat_all, all_sem.at[0], all_sem.at[1], partner)
+
+    @pl.when(lead)
+    def _():
+        stat_all[...] = collect(stat_x, x_peers, x_sem, per_device * tms * nz)
+        hand_over.start()
+
+    @pl.when(jnp.logical_not(lead))
+    def _():
+        hand_over.wait_recv()
+
+    final = stat_all[...]
     total = per_device * tms * nz * nx
     inv = lax.rsqrt(final[1:2] * (1.0 / total) + EPSILON)
     both = spread_groups(jnp.concatenate([final[0:1], inv] + [jnp.zeros((6, LANES), jnp.float32)], axis=0))
@@ -241,16 +262,19 @@
                 if 0 <= r - b < rows:
                     unfolded[(r - b) * width : (r - b + 1) * width, b * channels : (b + 1) * channels] = active
 
-    def multiply(src, unfolded):
+    def multiply(unfolded, product):
+        for owner in (0, 1):
+            part = slice(owner * 3 * block, (owner + 1) * 3 * block)
+            product[part] = lax.dot_general(
+                taps[part], unfolded[...], (((1,), (1,)), ((), ())), preferred_element_type=jnp.float32
+            )
+
+    def accumulate(src, product):
         frame = 2 * src + core
         totals = []
         for owner in (0, 1):
-            product = lax.dot_general(
-                taps[owner * 3 * block : (owner + 1) * 3 * block], unfolded[...], (((1,), (1,)), ((), ())),
-                preferred_element_type=jnp.float32,
-            )
             for a in range(3):
-                base = a * block
+                base = (owner * 3 + a) * block
                 one, two, three = (product[base + c * outs : base + (c + 1) * outs] for c in range(3))
                 one = jnp.where(at_left, 0.0, pltpu.roll(one, 1, 1))
                 three = jnp.where(at_right, 0.0, pltpu.roll(three, wide - 1, 1))
@@ -296,46 +320,59 @@
 
     late = [(step, chunk) for step in (half - 1, half) for chunk in ORDER]
     if ny >= 8:
-        events = {1: late[:1], 2: late[1:2], ny - 4: late[2:3], ny - 3: late[3:5], ny - 2: late[5:]}
+        events = {1: late[:1], 2: late[1:2], 3: late[2:3], 4: late[3:4], 5: late[4:5], ny - 1: late[5:]}
     else:
         events = {1: late[:3], ny - 1: late[3:]}
-
-    def stage(i, current, following):
-        if isinstance(i, int):
-            ring_events(events.get(i + 1, []))
+    wides, prods = (wide_a, wide_b), (prod_a, prod_b)
+
+    def arrivals(k):
+        if isinstance(k, int):
+            ring_events(events.get(k, []))
         else:
-            for k, todo in events.items():
-                pl.when(i + 1 == k)(functools.partial(ring_events, todo))
-        halo_wait(source(i + 1))
-        prepare(source(i + 1), following)
-        after(i, current)
-
-    def after(i, current):
-        src = source(i)
-        totals = multiply(src, current)
-        repeat_first(src, totals)
-        if isinstance(i, int):
-            if i > 0:
-                part_copy(released(i)).start()
-            if i > 1:
-                finish(released(i - 1))
-        else:
-            pl.when(i > 0)(lambda: part_copy(released(i)).start())
-            pl.when(i > 1)(lambda: finish(released(i - 1)))
-
-    halo_wait(source(0))
+            for when, todo in events.items():
+                pl.when(k == when)(functools.partial(ring_events, todo))
+        halo_wait(source(k))
+
+    def stage(i, parity):
+        other = 1 - parity
+        arrivals(i + 1)
+        prepare(source(i + 1), wides[other])
+        multiply(wides[parity], prods[parity])
+        sums(i - 1, other)
+        pl.when(i > 1)(lambda: part_copy(released(i - 1)).start())
+        pl.when(i > 2)(lambda: finish(released(i - 2)))
+
+    def sums(i, parity):
+        repeat_first(source(i), accumulate(source(i), prods[parity]))
+
+    arrivals(0)
     prepare(source(0), wide_a)
-
-    @pl.loop(0, half - 1)
+    arrivals(1)
+    prepare(source(1), wide_b)
+    multiply(wide_a, prod_a)
+
+    @pl.loop(0, half - 2)
     def _(p):
-        stage(2 * p, wide_a, wide_b)
-        stage(2 * p + 1, wide_b, wide_a)
-
-    stage(ny - 2, wide_a, wide_b)
-    after(ny - 1, wide_b)
+        stage(2 * p + 1, 1)
+        stage(2 * p + 2, 0)
+
+    stage(ny - 3, 1)
+    multiply(wide_a, prod_a)
+    sums(ny - 3, 1)
+    part_copy(released(ny - 3)).start()
+    if ny > 4:
+        finish(released(ny - 4))
+    sums(ny - 2, 0)
+    part_copy(released(ny - 2)).start()
+    arrivals(ny - 1)
+    finish(released(ny - 3))
+    prepare(source(ny - 1), wide_b)
+    multiply(wide_b, prod_b)
+    sums(ny - 1, 1)
+    part_copy(released(ny - 1)).start()
     part_copy(released(ny)).start()
-    finish(released(ny - 1))
-    finish(released(ny))
+    for j in range(ny - 2, ny + 1):
+        finish(released(j))
 
     several(result, tms - 1, back_sem).wait_recv()
     conv = jnp.transpose(result[:, :outs].reshape(channels, LANES).astype(jnp.float32), (1, 0))
@@ -345,9 +382,16 @@
     rest = jnp.transpose(rest, (1, 0))[:width]
     out[0, last] = rest.astype(out.dtype)
 
-    for buf, n, sem in ((stat_y, tms, y_sem), (stat_z, nz, z_sem), (stat_x, nx, x_sem), (ready, tms, back_sem)):
-        if n > 1:
-            several(buf, n - 1, sem).wait_send()
+    several(stat_y, tms - 1, y_sem).wait_send()
+    several(ready, tms - 1, back_sem).wait_send()
+
+    @pl.when(lead)
+    def _():
+        for buf, n, sem in ((stat_z, nz, z_sem), (stat_x, nx, x_sem)):
+            if n > 1:
+                several(buf, n - 1, sem).wait_send()
+        hand_over.wait_send()
+
     tap_remote.wait_send()
 
     def rows_out(n, sem):
@@ -381,6 +425,8 @@
             pltpu.VMEM((18 * outs, 3 * channels), bf16),
             pltpu.VMEM((wide, 3 * channels), bf16),
             pltpu.VMEM((wide, 3 * channels), bf16),
+            pltpu.VMEM((18 * outs, wide), f32),
+            pltpu.VMEM((18 * outs, wide), f32),
             pltpu.VMEM((2, tms + 2, outs, wide), f32),
             pltpu.VMEM((ny, 2, outs, wide), f32),
             pltpu.VMEM((tms, outs * 3 // 2, LANES), bf16),
@@ -389,11 +435,12 @@
             pltpu.VMEM((tms, 2, LANES), f32),
             pltpu.VMEM((nz, 2, LANES), f32),
             pltpu.VMEM((nx, 2, LANES), f32),
+            pltpu.VMEM((2, LANES), f32),
             pltpu.VMEM((8, channels), f32),
             dma((3,)), dma((2,)),
             dma, dma((ny, rows)),
             dma, dma((ny,)),
-            dma((2,)), dma((2,)), dma((2,)),
+            dma((2,)), dma((2,)), dma((2,)), dma((2,)),
             dma, dma((ny,)),
             dma((2,)),
         ],

time: 46 us -> 44.3 us (0.963)
  the two profiles are of different devices: /device:TPU:1 before, /device:TPU:73 now
where the time goes in v3:
time: 44.3 us; the launch traced here: 44.2 us
  Pallas kernels  43.4 us (98%)
  other arithmetic  0.74 us (2%)
    pallas_call x1, Pallas kernels, local(): pl.pallas_call(functools.partial(conv_kernel, sizes), out_shape=pltpu.VME...  43.4 us

profile of v3, /device:TPU:73, one launch (start us, length us, event | category | flops | bytes accessed | tf_op | source)
XLA Modules:
  0.0 44.2 jit_solution(805234301794939850)
XLA Ops:
  0.0 0.0 copy-start
  0.0 0.0 copy-start.1
  0.0 43.4 %fused_block.1 = bf16[1,3,64,512]{3,2,1,0:T(8,128)(2,1)S(1)} custom-call(bf16[1,3,64,512]{3,2,1,0:T(8,128)(2,1)} %feat.1, f32[1,512]{1,0:T(1,128)} %bitcast.6, f32[1,512]{1,0:T(1,128)} %bitcast.7, bf16[3,3,96,512]{3,2,1,0:T(8,128)(2,1)} %bitcast.5), custom_call_target="tpu_custom_call" | custom-call | tf_op jit(solution)/shard_map/fused_block/pallas_call | solution.py:418
  43.4 0.0 copy-done
  43.4 0.0 copy-done.1
  43.4 0.7 %add_convert_fusion = bf16[1,3,64,512]{3,2,1,0:T(8,128)(2,1)} fusion(bf16[1,3,64,512]{3,2,1,0:T(8,128)(2,1)S(1)} %fused_block.1, bf16[1,3,64,512]{3,2,1,0:T(8,128)(2,1)S(1)} %copy-done, f32[512]{0:T(512)S(1)} %copy-done.1), kind=kLoop, calls=%fused_computation | loop fusion | flops 491520 | bytes 591872 | tf_op jit(solution)/shard_map/convert_element_type | solution.py:450
Async XLA Ops:
  0.0 43.4 %copy-start = (bf16[1,3,64,512]{3,2,1,0:T(8,128)(2,1)S(1)}, bf16[1,3,64,512]{3,2,1,0:T(8,128)(2,1)}, u32[]{:S(2)}) copy-start(bf16[1,3,64,512]{3,2,1,0:T(8,128)(2,1)} %feat.1) | copy-start | bytes 589828
  0.0 43.4 %copy-start.1 = (f32[512]{0:T(512)S(1)}, f32[512]{0:T(512)}, u32[]{:S(2)}) copy-start(f32[512]{0:T(512)} %param.9) | copy-start | bytes 6148

commit v4 on v3

--- a/solution.py
+++ b/solution.py
@@ -15,6 +15,8 @@
 HIGHEST = lax.Precision.HIGHEST
 MESH = pl.DeviceIdType.MESH
 LANES = 128
+HEAD = 2
+PLAN = {1: (0, 1, 2), 2: (3,), 3: (4,), 7: (5,)}
 VMEM_LIMIT = 67043328 - 409600
 ORDER = (0, 2, 1)
 
@@ -23,7 +25,7 @@
     sizes, feat, gamma, beta, kern, out,
     frames, taps, wide_a, wide_b, prod_a, prod_b, acc, arrived, ready, result, consts, stat_y, stat_z, stat_x, stat_all,
     affine, local_sem, tap_sem, ring_send, ring_recv, halo_send, halo_recv,
-    y_sem, z_sem, x_sem, all_sem, part_send, part_recv, back_sem,
+    z_in, y_sem, z_sem, x_sem, all_sem, part_send, part_recv, back_sem,
 ):
     ny, nz, nx = sizes
     tms = 2 * ny
@@ -76,11 +78,14 @@
     def greet(device):
         pl.semaphore_signal(barrier, inc=1, device_id=device, device_id_type=MESH)
 
-    for peer in y_peers + z_peers + x_peers:
+    lead = core == 1
+    for k in far_first(nz):
+        pl.when(jnp.logical_and(lead, z + k < nz))(functools.partial(greet, {"rows_0": z + k}))
+    for peer in y_peers + x_peers:
         greet(peer)
     crosses_up = jnp.logical_and(has_up, x == 0)
     crosses_down = jnp.logical_and(has_down, x == nx - 1)
-    expected = len(y_peers) + len(z_peers) + len(x_peers)
+    expected = len(y_peers) + len(x_peers) + jnp.where(lead, z, 0)
     if nx > 1:
         pl.when(crosses_up)(lambda: greet(up))
         pl.when(crosses_down)(lambda: greet(down))
@@ -125,6 +130,12 @@
     stat_y[me] = jnp.concatenate([mean_g[0:1], m2_g[0:1]], axis=0)
 
     pl.semaphore_wait(barrier, expected)
+    for k in far_first(nz):
+
+        @pl.when(jnp.logical_and(lead, z - k >= 0))
+        def _():
+            pl.semaphore_signal(z_in, inc=1, device_id={"rows_0": z - k}, device_id_type=MESH)
+
 
     def publish(buf, at, peers, sem):
         for peer in peers:
@@ -196,12 +207,12 @@
             ring_event(step, chunk)
 
     ring_events(early[:1])
-    lead = core == 1
     span = collect(stat_y, y_peers, y_sem, per_device)
 
     @pl.when(lead)
     def _():
         stat_z[z] = span
+        pl.when(z < nz - 1)(lambda: pl.semaphore_wait(z_in, nz - 1 - z))
         publish(stat_z, z, z_peers, z_sem)
 
     ring_events(early[1:4])
@@ -211,7 +222,8 @@
         stat_x[x] = collect(stat_z, z_peers, z_sem, per_device * tms)
         publish(stat_x, x, x_peers, x_sem)
 
-    ring_events(early[4:])
+    late = [(step, chunk) for step in (half - 1, half) for chunk in ORDER]
+    ring_events(early[4:] + late[: HEAD if ny >= 8 else 0])
     hand_over = remote(stat_all, stat_all, all_sem.at[0], all_sem.at[1], partner)
 
     @pl.when(lead)
@@ -318,9 +330,9 @@
                 ready[2 * to + which] = value
                 remote(ready.at[2 * to + which], result.at[me], back_sem.at[0], back_sem.at[1], {"tm_0": to, "tm_1": which}).start()
 
-    late = [(step, chunk) for step in (half - 1, half) for chunk in ORDER]
     if ny >= 8:
-        events = {1: late[:1], 2: late[1:2], 3: late[2:3], 4: late[3:4], 5: late[4:5], ny - 1: late[5:]}
+        events = {k: [late[e] for e in todo if e >= HEAD] for k, todo in PLAN.items()}
+        events = {k: todo for k, todo in events.items() if todo}
     else:
         events = {1: late[:3], ny - 1: late[3:]}
     wides, prods = (wide_a, wide_b), (prod_a, prod_b)
@@ -365,9 +377,9 @@
     sums(ny - 2, 0)
     part_copy(released(ny - 2)).start()
     arrivals(ny - 1)
-    finish(released(ny - 3))
     prepare(source(ny - 1), wide_b)
     multiply(wide_b, prod_b)
+    finish(released(ny - 3))
     sums(ny - 1, 1)
     part_copy(released(ny - 1)).start()
     part_copy(released(ny)).start()
@@ -440,6 +452,7 @@
             dma((3,)), dma((2,)),
             dma, dma((ny, rows)),
             dma, dma((ny,)),
+            pltpu.SemaphoreType.REGULAR,
             dma((2,)), dma((2,)), dma((2,)), dma((2,)),
             dma, dma((ny,)),
             dma((2,)),

time: 44.3 us -> 42.5 us (0.959)
  the two profiles are of different devices: /device:TPU:73 before, /device:TPU:1 now
where the time goes in v4:
time: 42.5 us; the launch traced here: 42.4 us
  Pallas kernels  41.6 us (98%)
  other arithmetic  0.74 us (2%)
    pallas_call x1, Pallas kernels, local(): pl.pallas_call(functools.partial(conv_kernel, sizes), out_shape=pltpu.VME...  41.6 us

profile of v4, /device:TPU:1, one launch (start us, length us, event | category | flops | bytes accessed | tf_op | source)
XLA Modules:
  0.0 42.4 jit_solution(12965227382001475133)
XLA Ops:
  0.0 0.0 copy-start
  0.0 0.0 copy-start.1
  0.0 41.6 %fused_block.1 = bf16[1,3,64,512]{3,2,1,0:T(8,128)(2,1)S(1)} custom-call(bf16[1,3,64,512]{3,2,1,0:T(8,128)(2,1)} %feat.1, f32[1,512]{1,0:T(1,128)} %bitcast.6, f32[1,512]{1,0:T(1,128)} %bitcast.7, bf16[3,3,96,512]{3,2,1,0:T(8,128)(2,1)} %bitcast.5), custom_call_target="tpu_custom_call" | custom-call | tf_op jit(solution)/shard_map/fused_block/pallas_call | solution.py:430
  41.6 0.0 copy-done
  41.6 0.0 copy-done.1
  41.6 0.7 %add_convert_fusion = bf16[1,3,64,512]{3,2,1,0:T(8,128)(2,1)} fusion(bf16[1,3,64,512]{3,2,1,0:T(8,128)(2,1)S(1)} %fused_block.1, bf16[1,3,64,512]{3,2,1,0:T(8,128)(2,1)S(1)} %copy-done, f32[512]{0:T(512)S(1)} %copy-done.1), kind=kLoop, calls=%fused_computation | loop fusion | flops 491520 | bytes 591872 | tf_op jit(solution)/shard_map/convert_element_type | solution.py:463
Async XLA Ops:
  0.0 41.6 %copy-start = (bf16[1,3,64,512]{3,2,1,0:T(8,128)(2,1)S(1)}, bf16[1,3,64,512]{3,2,1,0:T(8,128)(2,1)}, u32[]{:S(2)}) copy-start(bf16[1,3,64,512]{3,2,1,0:T(8,128)(2,1)} %feat.1) | copy-start | bytes 589828
  0.0 41.6 %copy-start.1 = (f32[512]{0:T(512)S(1)}, f32[512]{0:T(512)}, u32[]{:S(2)}) copy-start(f32[512]{0:T(512)} %param.9) | copy-start | bytes 6148

commit v5 on v4

--- a/solution.py
+++ b/solution.py
@@ -23,9 +23,9 @@
 
 def conv_kernel(
     sizes, feat, gamma, beta, kern, out,
-    frames, taps, wide_a, wide_b, prod_a, prod_b, acc, arrived, ready, result, consts, stat_y, stat_z, stat_x, stat_all,
+    frames, taps, wide_a, wide_b, prod_a, prod_b, acc, arrived, ready, result, consts, stat_y, stat_z, stat_x,
     affine, local_sem, tap_sem, ring_send, ring_recv, halo_send, halo_recv,
-    z_in, y_sem, z_sem, x_sem, all_sem, part_send, part_recv, back_sem,
+    z_in, y_sem, z_sem, x_sem, part_send, part_recv, back_sem,
 ):
     ny, nz, nx = sizes
     tms = 2 * ny
@@ -73,7 +73,7 @@
 
     y_peers = [{"tm_0": chip(k), "tm_1": c} for k in far_first(ny) for c in (core, 1 - core)] + [partner]
     z_peers = [{"rows_0": wrap(z + k, nz)} for k in far_first(nz)]
-    x_peers = [{"rows_1": wrap(x + k, nx)} for k in far_first(nx)]
+    x_peers = [{"rows_1": wrap(x + k, nx), "tm_1": c} for k in far_first(nx) for c in (1 - core, core)]
 
     def greet(device):
         pl.semaphore_signal(barrier, inc=1, device_id=device, device_id_type=MESH)
@@ -215,27 +215,19 @@
         pl.when(z < nz - 1)(lambda: pl.semaphore_wait(z_in, nz - 1 - z))
         publish(stat_z, z, z_peers, z_sem)
 
-    ring_events(early[1:4])
+    ring_events(early[1:])
 
     @pl.when(lead)
     def _():
         stat_x[x] = collect(stat_z, z_peers, z_sem, per_device * tms)
-        publish(stat_x, x, x_peers, x_sem)
+        publish(stat_x, x, x_peers + [partner], x_sem)
 
     late = [(step, chunk) for step in (half - 1, half) for chunk in ORDER]
-    ring_events(early[4:] + late[: HEAD if ny >= 8 else 0])
-    hand_over = remote(stat_all, stat_all, all_sem.at[0], all_sem.at[1], partner)
-
-    @pl.when(lead)
-    def _():
-        stat_all[...] = collect(stat_x, x_peers, x_sem, per_device * tms * nz)
-        hand_over.start()
-
-    @pl.when(jnp.logical_not(lead))
-    def _():
-        hand_over.wait_recv()
-
-    final = stat_all[...]
+    ring_events(late[: HEAD if ny >= 8 else 0])
+    if nx > 1:
+        pl.when(lead)(lambda: several(stat_x, nx - 1, x_sem).wait_recv())
+    pl.when(jnp.logical_not(lead))(lambda: several(stat_x, nx, x_sem).wait_recv())
+    final = collect(stat_x, (), x_sem, per_device * tms * nz)
     total = per_device * tms * nz * nx
     inv = lax.rsqrt(final[1:2] * (1.0 / total) + EPSILON)
     both = spread_groups(jnp.concatenate([final[0:1], inv] + [jnp.zeros((6, LANES), jnp.float32)], axis=0))
@@ -399,10 +391,8 @@
 
     @pl.when(lead)
     def _():
-        for buf, n, sem in ((stat_z, nz, z_sem), (stat_x, nx, x_sem)):
-            if n > 1:
-                several(buf, n - 1, sem).wait_send()
-        hand_over.wait_send()
+        several(stat_z, nz - 1, z_sem).wait_send()
+        several(stat_y, 2 * nx - 1, x_sem).wait_send()
 
     tap_remote.wait_send()
 
@@ -447,13 +437,12 @@
             pltpu.VMEM((tms, 2, LANES), f32),
             pltpu.VMEM((nz, 2, LANES), f32),
             pltpu.VMEM((nx, 2, LANES), f32),
-            pltpu.VMEM((2, LANES), f32),
             pltpu.VMEM((8, channels), f32),
             dma((3,)), dma((2,)),
             dma, dma((ny, rows)),
             dma, dma((ny,)),
             pltpu.SemaphoreType.REGULAR,
-            dma((2,)), dma((2,)), dma((2,)), dma((2,)),
+            dma((2,)), dma((2,)), dma((2,)),
             dma, dma((ny,)),
             dma((2,)),
         ],

time: 42.5 us -> 41.8 us (0.984)
  Pallas kernels: 41.6 us -> 40.9 us
    pallas_call x1, Pallas kernels: 41.6 us -> 40.9 us  [local(): pl.pallas_call(functools.partial(conv_kernel, sizes), out_shape=pltpu.VME...]
where the time goes in v5:
time: 41.8 us; the launch traced here: 41.7 us
  Pallas kernels  40.9 us (98%)
  other arithmetic  0.74 us (2%)
    pallas_call x1, Pallas kernels, local(): pl.pallas_call(functools.partial(conv_kernel, sizes), out_shape=pltpu.VME...  40.9 us

profile of v5, /device:TPU:1, one launch (start us, length us, event | category | flops | bytes accessed | tf_op | source)
XLA Modules:
  0.0 41.7 jit_solution(16478074217877774529)
XLA Ops:
  0.0 0.0 copy-start
  0.0 0.0 copy-start.1
  0.0 40.9 %fused_block.1 = bf16[1,3,64,512]{3,2,1,0:T(8,128)(2,1)S(1)} custom-call(bf16[1,3,64,512]{3,2,1,0:T(8,128)(2,1)} %feat.1, f32[1,512]{1,0:T(1,128)} %bitcast.6, f32[1,512]{1,0:T(1,128)} %bitcast.7, bf16[3,3,96,512]{3,2,1,0:T(8,128)(2,1)} %bitcast.5), custom_call_target="tpu_custom_call" | custom-call | tf_op jit(solution)/shard_map/fused_block/pallas_call | solution.py:420
  40.9 0.0 copy-done
  40.9 0.0 copy-done.1
  40.9 0.7 %add_convert_fusion = bf16[1,3,64,512]{3,2,1,0:T(8,128)(2,1)} fusion(bf16[1,3,64,512]{3,2,1,0:T(8,128)(2,1)S(1)} %fused_block.1, bf16[1,3,64,512]{3,2,1,0:T(8,128)(2,1)S(1)} %copy-done, f32[512]{0:T(512)S(1)} %copy-done.1), kind=kLoop, calls=%fused_computation | loop fusion | flops 491520 | bytes 591872 | tf_op jit(solution)/shard_map/convert_element_type | solution.py:452
Async XLA Ops:
  0.0 40.9 %copy-start = (bf16[1,3,64,512]{3,2,1,0:T(8,128)(2,1)S(1)}, bf16[1,3,64,512]{3,2,1,0:T(8,128)(2,1)}, u32[]{:S(2)}) copy-start(bf16[1,3,64,512]{3,2,1,0:T(8,128)(2,1)} %feat.1) | copy-start | bytes 589828
  0.0 40.9 %copy-start.1 = (f32[512]{0:T(512)S(1)}, f32[512]{0:T(512)}, u32[]{:S(2)}) copy-start(f32[512]{0:T(512)} %param.9) | copy-start | bytes 6148

commit v6 on v5

--- a/solution.py
+++ b/solution.py
@@ -15,8 +15,8 @@
 HIGHEST = lax.Precision.HIGHEST
 MESH = pl.DeviceIdType.MESH
 LANES = 128
-HEAD = 2
-PLAN = {1: (0, 1, 2), 2: (3,), 3: (4,), 7: (5,)}
+HEAD = 3
+PLAN = {1: (3,), 2: (4,), 7: (5,)}
 VMEM_LIMIT = 67043328 - 409600
 ORDER = (0, 2, 1)
 
@@ -364,10 +364,10 @@
     multiply(wide_a, prod_a)
     sums(ny - 3, 1)
     part_copy(released(ny - 3)).start()
+    sums(ny - 2, 0)
+    part_copy(released(ny - 2)).start()
     if ny > 4:
         finish(released(ny - 4))
-    sums(ny - 2, 0)
-    part_copy(released(ny - 2)).start()
     arrivals(ny - 1)
     prepare(source(ny - 1), wide_b)
     multiply(wide_b, prod_b)

time: 41.8 us -> 41.7 us (level)
  no operation moved by 1% of the time
where the time goes in v6:
time: 41.7 us; the launch traced here: 41.6 us
  Pallas kernels  40.8 us (98%)
  other arithmetic  0.74 us (2%)
    pallas_call x1, Pallas kernels, local(): pl.pallas_call(functools.partial(conv_kernel, sizes), out_shape=pltpu.VME...  40.8 us

profile of v6, /device:TPU:1, one launch (start us, length us, event | category | flops | bytes accessed | tf_op | source)
XLA Modules:
  0.0 41.6 jit_solution(18416106742940299380)
XLA Ops:
  0.0 0.0 copy-start
  0.0 0.0 copy-start.1
  0.0 40.8 %fused_block.1 = bf16[1,3,64,512]{3,2,1,0:T(8,128)(2,1)S(1)} custom-call(bf16[1,3,64,512]{3,2,1,0:T(8,128)(2,1)} %feat.1, f32[1,512]{1,0:T(1,128)} %bitcast.6, f32[1,512]{1,0:T(1,128)} %bitcast.7, bf16[3,3,96,512]{3,2,1,0:T(8,128)(2,1)} %bitcast.5), custom_call_target="tpu_custom_call" | custom-call | tf_op jit(solution)/shard_map/fused_block/pallas_call | solution.py:420
  40.8 0.0 copy-done
  40.8 0.0 copy-done.1
  40.9 0.7 %add_convert_fusion = bf16[1,3,64,512]{3,2,1,0:T(8,128)(2,1)} fusion(bf16[1,3,64,512]{3,2,1,0:T(8,128)(2,1)S(1)} %fused_block.1, bf16[1,3,64,512]{3,2,1,0:T(8,128)(2,1)S(1)} %copy-done, f32[512]{0:T(512)S(1)} %copy-done.1), kind=kLoop, calls=%fused_computation | loop fusion | flops 491520 | bytes 591872 | tf_op jit(solution)/shard_map/convert_element_type | solution.py:452
Async XLA Ops:
  0.0 40.8 %copy-start = (bf16[1,3,64,512]{3,2,1,0:T(8,128)(2,1)S(1)}, bf16[1,3,64,512]{3,2,1,0:T(8,128)(2,1)}, u32[]{:S(2)}) copy-start(bf16[1,3,64,512]{3,2,1,0:T(8,128)(2,1)} %feat.1) | copy-start | bytes 589828
  0.0 40.8 %copy-start.1 = (f32[512]{0:T(512)S(1)}, f32[512]{0:T(512)}, u32[]{:S(2)}) copy-start(f32[512]{0:T(512)} %param.9) | copy-start | bytes 6148
